TPU v7x, 256 devices: a whole 4x4x8 slice. The times are simulated.
256 devices in a mesh: dp: 64 (over z, x, core), tensor: 4 (over y).
Axes of the slice: x: 4, y: 4, z: 8, core: 2. Of those that a mesh axis runs over, the one named last changes fastest.
Arguments:
- master_old: float32 [3072, 36864], P('dp', 'tensor'), may hold values from -6 to 6
- moment1_old: float32 [3072, 36864], P('dp', 'tensor'), may hold values from -4 to 4
- moment2_old: float32 [3072, 36864], P('dp', 'tensor'), may hold values from 0.0001 to 1
- grad: bfloat16 [3072, 36864], P('dp', 'tensor'), may hold values from -28 to 28
- send_slots: int32 [64, 1728], P('dp'), may hold values from 0 to 1727, each once within a row
- recv_slots: int32 [64, 1728], P('dp'), may hold values from 0 to 1727, each once within a row
Outputs:
- master_new: float32 [3072, 36864], P('dp', 'tensor')
- moment1_new: float32 [3072, 36864], P('dp', 'tensor')
- moment2_new: float32 [3072, 36864], P('dp', 'tensor')
Inputs may be any that keep to these rules, and one draw needn't show every extreme that they name: `send_slots`: each row is a permutation of 0 to 1727; entry [i, j * 27 + q] is the old slot of the q-th block that device i of dp sends to device j. `recv_slots`: each row is a permutation of 0 to 1727; entry [j, i * 27 + q] is the new slot on device j of the q-th block from device i.
All inputs are finite; a program needn't handle non-finite values.
Results may differ from a plain program's by a relative error of at most 0.0003.
Values sent between devices are 32-bit elements; how exact they have to be, the bound alone decides.
A program may use at most 64 MiB of HBM per device.

v0:
```python
import functools

import jax
import jax.numpy as jnp
from jax import lax
from jax.sharding import Mesh
from jax.sharding import PartitionSpec as P

ROWS = 3072
FF = 36864
SEGW = 128
DP = ("dp_0", "dp_1", "dp_2")
DP_TENSOR = ("dp_0", "dp_1", "dp_2", "tensor")


beta_one = 0.9
beta_two = 0.95
correct_one = 0.6513215599
correct_two = 0.4012630608
adam_eps = 1e-08
learning_rate = 0.01
weight_decay = 0.1
clip_ratio = 0.75


def one_axis_at_a_time(value, axes):
    return functools.reduce(lax.psum, axes, value)


def swapped(block, axis, apart):
    count = lax.axis_size(axis)
    route = []
    for low in range(count):
        high = low | 1 << apart
        if high != low and high < count:
            route += [(low, high), (high, low)]
    return lax.ppermute(block, axis, route)


def per_device(master_old, moment1_old, moment2_old, grad, send_slots, recv_slots):
    rows_here, columns = master_old.shape
    half_width = columns // 2
    segments = half_width // SEGW
    blocks = rows_here * segments
    devices = lax.axis_size(DP)
    per_peer = blocks // devices
    is_even = lax.axis_index("tensor") % 2 == 0
    wide = grad.astype(jnp.float32)
    sum_squares = one_axis_at_a_time(jnp.sum(wide * wide), DP_TENSOR)
    stacked = jnp.stack([master_old, moment1_old, moment2_old], 0)
    tiled = (
        stacked.reshape(3, rows_here, 2, segments, SEGW)
        .transpose(0, 1, 3, 2, 4)
        .reshape(3, blocks, 2, SEGW)
    )
    own_send = send_slots[0]
    own_recv = recv_slots[0]
    outgoing = jnp.take(tiled, own_send, axis=1).reshape(3, devices, per_peer, 2, SEGW)
    arrived = lax.all_to_all(outgoing, DP, split_axis=1, concat_axis=1, tiled=True).reshape(
        3, blocks, 2, SEGW
    )
    inverse = jnp.zeros((blocks,), jnp.int32).at[own_recv].set(jnp.arange(blocks, dtype=jnp.int32))
    tiles = jnp.take(arrived, inverse, axis=1)
    first = tiles[..., 0, :]
    second = tiles[..., 1, :]
    kept = jnp.where(is_even, first, second)
    outgoing = jnp.where(is_even, second, first)
    arrived = swapped(outgoing, "tensor", 0)
    moved = jnp.where(is_even, jnp.stack([kept, arrived], -2), jnp.stack([arrived, kept], -2))
    placed = (
        moved.reshape(3, rows_here, segments, 2, SEGW)
        .transpose(0, 1, 3, 2, 4)
        .reshape(3, rows_here, columns)
    )
    new_master = placed[0]
    new_first = placed[1]
    new_second = placed[2]
    limit = clip_ratio * jnp.sqrt(jnp.float32(ROWS * FF))
    clip_scale = jnp.minimum(1.0, limit / jnp.sqrt(sum_squares + 1e-06))
    scaled = clip_scale * wide
    moment1 = beta_one * new_first + (1.0 - beta_one) * scaled
    moment2 = beta_two * new_second + (1.0 - beta_two) * scaled * scaled
    update = moment1 / correct_one / (jnp.sqrt(moment2 / correct_two) + adam_eps)
    master = new_master - learning_rate * (update + weight_decay * new_master)
    return (master, moment1, moment2)


def solution(mesh):
    split = Mesh(
        mesh.devices.reshape(8, 4, 2, mesh.shape["tensor"]), ("dp_0", "dp_1", "dp_2", "tensor")
    )
    return jax.shard_map(
        per_device,
        mesh=split,
        in_specs=(
            P(DP, "tensor"),
            P(DP, "tensor"),
            P(DP, "tensor"),
            P(DP, "tensor"),
            P(DP, None),
            P(DP, None),
        ),
        out_specs=(P(DP, "tensor"), P(DP, "tensor"), P(DP, "tensor")),
        check_vma=False,
    )
```

profile of v0, /device:TPU:1, one launch (start us, length us, event | category | flops | bytes accessed | tf_op | source)
XLA Modules:
  0.0 299.1 jit_solution(16645460600656540258)
XLA Ops:
  1.4 1.6 stack.28
  3.0 2.8 stack.27
  5.7 2.7 stack.26
  8.5 2.6 maximum_bitcast_fusion
  11.1 5.0 %copy.37 = f32[3,48,36,2,128]{4,3,2,1,0:T(2,128)} copy(f32[3,48,36,2,128]{4,2,3,1,0:T(8,128)S(1)} %maximum_bitcast_fusion) | data formatting | bytes 10616832 | tf_op jit(solution)/shard_map/transpose | solution.py:53
  16.1 15.3 %gather_fusion = f32[1728,3,2,128]{3,2,1,0:T(2,128)} fusion(f32[3,1728,2,128]{3,2,1,0:T(2,128)} %bitcast.18, s32[2048]{0:T(1024)S(1)} %pad_clamp_fusion.1), kind=kCustom, calls=%fused_computation.clone | custom fusion | bytes 10623744 | tf_op jit(solution)/shard_map/jit(_take)/gather | solution.py:58
  31.5 8.1 %broadcast_select_fusion = f32[1728,3,2,128]{3,2,1,0:T(2,128)S(1)} fusion(f32[1728,3,2,128]{3,2,1,0:T(2,128)} %gather_fusion, pred[1728]{0:T(1024)(128)(4,1)S(1)} %compare_and_fusion.1), kind=kLoop, calls=%fused_computation.7 | loop fusion | flops 1327104 | bytes 10618560 | tf_op jit(solution)/shard_map/jit(_take)/select_n | solution.py:58
  39.5 4.2 %copy.38 = f32[3,64,27,2,128]{4,3,2,0,1:T(2,128)} copy(f32[3,64,27,2,128]{4,3,0,2,1:T(2,128)S(1)} %bitcast.19) | data formatting | bytes 10616832 | tf_op jit(solution)/shard_map/reshape | solution.py:58
  43.7 13.5 %all-to-all-start = ((f32[3,64,27,2,128]{4,3,2,0,1:T(2,128)}), f32[3,64,27,2,128]{4,3,2,0,1:T(2,128)}, u32[]{:S(2)}, u32[]{:S(2)}) async-start(f32[3,64,27,2,128]{4,3,2,0,1:T(2,128)} %copy.38), calls=%async_computation | async-start | bytes 10616832 | tf_op jit(solution)/shard_map/all_to_all | solution.py:59
  57.2 8.8 %scatter_custom_fusion = s32[1728]{0:T(1024)S(1)} fusion(s32[1728]{0:T(1024)S(1)} %fusion.5, s32[1728]{0:T(1024)S(1)} %iota.3, s32[]{:T(128)} %constant.26.clone.1), kind=kCustom, calls=%fused_computation.29 | custom fusion | bytes 6916 | tf_op jit(solution)/shard_map/scatter | solution.py:62
  66.1 109.1 %all-to-all-done = f32[3,64,27,2,128]{4,3,2,0,1:T(2,128)} async-done(((f32[3,64,27,2,128]{4,3,2,0,1:T(2,128)}), f32[3,64,27,2,128]{4,3,2,0,1:T(2,128)}, u32[]{:S(2)}, u32[]{:S(2)}) %all-to-all-start) | async-done | bytes 5308448 | tf_op jit(solution)/shard_map/all_to_all | solution.py:59
  175.2 6.7 %copy.39 = f32[3,64,27,2,128]{4,3,2,1,0:T(2,128)} copy(f32[3,64,27,2,128]{4,3,2,0,1:T(2,128)} %all-to-all-done) | data formatting | bytes 10616832 | tf_op jit(solution)/shard_map/all_to_all | solution.py:59
  181.9 15.4 %gather_fusion.1 = f32[1728,3,2,128]{3,2,1,0:T(2,128)} fusion(f32[3,1728,2,128]{3,2,1,0:T(2,128)} %bitcast.17, s32[2048]{0:T(1024)S(1)} %pad_clamp_fusion), kind=kCustom, calls=%fused_computation.1.clone | custom fusion | bytes 10623744 | tf_op jit(solution)/shard_map/jit(_take)/gather | solution.py:63
  197.2 8.1 %select_bitcast_fusion = f32[3,1728,2,128]{3,2,0,1:T(2,128)S(1)} fusion(f32[1728,3,2,128]{3,2,1,0:T(2,128)} %gather_fusion.1, pred[1728]{0:T(1024)(128)(4,1)S(1)} %compare_and_fusion), kind=kLoop, calls=%fused_computation.6 | loop fusion | flops 1327104 | bytes 10618560 | tf_op jit(solution)/shard_map/jit(_take)/select_n | solution.py:63
  205.3 3.9 %broadcast_select_fusion.2 = (f32[3,1728,1,128]{3,2,0,1:T(1,128)S(1)}, f32[3,1728,1,128]{3,2,0,1:T(1,128)S(1)}) fusion(pred[]{:T(512)S(6)} %eq.5, f32[3,1728,2,128]{3,2,0,1:T(2,128)S(1)} %select_bitcast_fusion), kind=kLoop, calls=%fused_computation.9 | loop fusion | flops 1327104 | bytes 10616833 | tf_op jit(solution)/shard_map/jit(_where)/select_n | solution.py:66
  209.2 1.7 copy.50
  210.9 1.3 collective-permute-start
  213.3 13.7 %psum.28 = f32[]{:T(128)} all-reduce(f32[]{:T(128)} %fusion.3), channel_id=1, replica_groups=mesh['dp_0'=8,'dp_1'=4,'dp_2'=2,'tensor'=4] {'dp_0'}, use_global_device_ids=true, to_apply=%region_2.4 | all-reduce | flops 1 | bytes 8 | tf_op jit(solution)/shard_map/psum | solution.py:27
  227.0 9.4 %psum.29 = f32[]{:T(128)} all-reduce(f32[]{:T(128)} %psum.28), channel_id=1, replica_groups=mesh['dp_0'=8,'dp_1'=4,'dp_2'=2,'tensor'=4] {'dp_1'}, use_global_device_ids=true, to_apply=%region_3.5 | all-reduce | flops 1 | bytes 8 | tf_op jit(solution)/shard_map/psum | solution.py:27
  236.4 9.2 %psum.30 = f32[]{:T(128)} all-reduce(f32[]{:T(128)} %psum.29), channel_id=1, replica_groups=mesh['dp_0'=8,'dp_1'=4,'dp_2'=2,'tensor'=4] {'dp_2'}, use_global_device_ids=true, to_apply=%region_4.6 | all-reduce | flops 1 | bytes 8 | tf_op jit(solution)/shard_map/psum | solution.py:27
  245.6 26.5 %psum.31 = f32[]{:T(128)} all-reduce(f32[]{:T(128)} %psum.30), channel_id=1, replica_groups=mesh['dp_0'=8,'dp_1'=4,'dp_2'=2,'tensor'=4] {'tensor'}, use_global_device_ids=true, to_apply=%region_5.7 | all-reduce | flops 1 | bytes 8 | tf_op jit(solution)/shard_map/psum | solution.py:27
  272.7 2.7 copy.40
  275.4 1.7 copy.42
  277.2 2.5 stack.31
  280.2 1.3 copy-done
  282.1 2.2 slice_multiply_fusion
  284.9 1.5 squeeze.15
  286.3 2.1 copy.47
  288.4 1.5 mul.50
  289.9 2.1 copy.48
  291.9 1.5 mul.57
  293.4 5.7 %multiply_subtract_fusion = (f32[48,9216]{1,0:T(8,128)}, f32[48,9216]{1,0:T(8,128)}, f32[48,9216]{1,0:T(8,128)}) fusion(f32[48,9216]{1,0:T(8,128)} %squeeze.15, f32[48,9216]{1,0:T(8,128)} %mul.50, bf16[48,9216]{1,0:T(8,128)(2,1)S(1)} %copy-done.2, f32[]{:T(128)S(6)} %min_shard_map.3, f32[48,9216]{1,0:T(8,128)} %mul.57), kind=kLoop, calls=%fused_computation.20 | loop fusion | flops 6635520 | bytes 11501572 | tf_op jit(solution)/shard_map/sub | solution.py:84
  (21 shorter events, 3.5 us)
Async XLA Ops:
  43.7 13.5 %copy-start.3 = (s32[1,1728]{1,0:T(1,128)S(1)}, s32[1,1728]{1,0:T(1,128)}, u32[]{:S(2)}) copy-start(s32[1,1728]{1,0:T(1,128)} %param.13) | copy-start | bytes 20740
  43.7 131.5 %all-to-all-start = ((f32[3,64,27,2,128]{4,3,2,0,1:T(2,128)}), f32[3,64,27,2,128]{4,3,2,0,1:T(2,128)}, u32[]{:S(2)}, u32[]{:S(2)}) async-start(f32[3,64,27,2,128]{4,3,2,0,1:T(2,128)} %copy.38), calls=%async_computation | async-start | bytes 10616832 | tf_op jit(solution)/shard_map/all_to_all | solution.py:59
  209.2 3.0 %copy-start.1 = (bf16[48,9216]{1,0:T(8,128)(2,1)S(1)}, bf16[48,9216]{1,0:T(8,128)(2,1)}, u32[]{:S(2)}) copy-start(bf16[48,9216]{1,0:T(8,128)(2,1)} %param.11) | copy-start | bytes 2654212
  210.9 66.3 %collective-permute-start = (f32[3,1728,128]{2,1,0:T(8,128)}, f32[3,1728,128]{2,1,0:T(8,128)}, u32[]{:S(2)}, u32[]{:S(2)}) collective-permute-start(f32[3,1728,128]{2,1,0:T(8,128)} %bitcast.16), channel_id=1, source_target_pairs={{0,1},{1,0},{2,3},{3,2},{4,5},{5,4},{6,7},{7,6},{8,9},{9,8},{10,11... | collective-permute-start | bytes 7962632 | tf_op jit(solution)/shard_map/ppermute | solution.py:37
  279.7 1.8 copy-start
  291.9 1.5 copy-start.2
where the time goes:
time: 304 us; the launch traced here: 299 us
  waiting for transfers between devices  109 us (36%)
  local copies, waits for them, and re-layouts  81.9 us (27%)
  blocking collectives  58.8 us (19%)
  other arithmetic  33 us (11%)
  starting transfers between devices  14.7 us (5%)
    all_to_all x1, waiting for transfers between devices, per_device(): lax.all_to_all(outgoing, DP, split_axis=1, concat_axis=1, tiled=True)  109 us
    psum x4, blocking collectives, one_axis_at_a_time(): return functools.reduce(lax.psum, axes, value)  58.8 us
    gather x1, local copies, waits for them, and re-layouts, per_device(): tiles = jnp.take(arrived, inverse, axis=1)  15.4 us
    gather x1, local copies, waits for them, and re-layouts, per_device(): jnp.take(tiled, own_send, axis=1).reshape(3, devices, per_peer, 2, SEGW)  15.3 us
    all_to_all x1, starting transfers between devices, per_device(): lax.all_to_all(outgoing, DP, split_axis=1, concat_axis=1, tiled=True)  13.5 us
    scatter x1, local copies, waits for them, and re-layouts, per_device(): jnp.zeros((blocks,), jnp.int32).at[own_recv]  8.77 us
    select_n x2, other arithmetic, per_device(): jnp.take(tiled, own_send, axis=1).reshape(3, devices, per_peer, 2, SEGW)  8.07 us
    select_n x2, other arithmetic, per_device(): tiles = jnp.take(arrived, inverse, axis=1)  8.07 us
  transfers between devices with their start and end apart: 2, of which 1 were waited for; matrix products, arithmetic and copies ran while one was open for 5% of the time, Pallas kernels for 0%

commit v1 on v0

v1 whole, which is shorter than its diff:
```python
import functools

import jax
import jax.numpy as jnp
from jax import lax
from jax.experimental import pallas as pl
from jax.experimental.pallas import tpu as pltpu
from jax.sharding import PartitionSpec as P

ROWS = 3072
FF = 36864
SEGW = 128
RD = 48
COLS = 9216
HALF = 4608
NSEG = 36
BLOCKS = 1728
N_DP = 64
PER_PEER = 27
TILES = 2 * BLOCKS
MESH = pl.DeviceIdType.MESH

beta_one = 0.9
beta_two = 0.95
correct_one = 0.6513215599
correct_two = 0.4012630608
adam_eps = 1e-08
learning_rate = 0.01
weight_decay = 0.1
clip_ratio = 0.75

CHUNK = 512


def kernel(
    send_ref, place_ref, first_hbm, second_hbm, master_hbm, grad_hbm,
    first_out, second_out, master_out,
    old0, old1, old2, send0, send1, send2, recv0, recv1, recv2, new0, new1, new2,
    grad, update, pair_rows, own_row, all_rows, inverse, inverse_smem,
    load_sems, out_sems, send_sem, recv_sems, small_send, small_recv, table_sem,
):
    me = lax.axis_index("dp")
    shard = lax.axis_index("tensor")
    z, x, core = me // 8, (me // 2) % 4, me % 2
    parity = shard % 2
    even_shard = shard - parity
    olds, sends, recvs, news = (old0, old1, old2), (send0, send1, send2), (recv0, recv1, recv2), (new0, new1, new2)
    outs = (first_out, second_out, master_out)

    def peer_of(n):
        zi, xi = n % 8, (n // 8) % 4
        other_shard, other_core = 1 - (n // 32) % 2, 1 - n // 64
        dz = jnp.where(zi % 2 == 0, 4 + zi // 2, 3 - zi // 2)
        jz = (z + dz) % 8
        jx = (x + xi + 1) % 4
        jc = (core + other_core) % 2
        half = (parity + other_shard) % 2
        return (jz * 4 + jx) * 2 + jc, half

    barrier = pltpu.get_barrier_semaphore()

    @pl.loop(0, 127)
    def _(n):
        j, half = peer_of(n)
        pl.semaphore_signal(barrier, inc=1, device_id=(j, even_shard + half), device_id_type=MESH)

    far_shards = [(shard + k) % 4 for k in (1, 2, 3)]
    for k in (1, 2, 3):
        pl.semaphore_signal(barrier, inc=1, device_id=(me, (shard + k) % 4), device_id_type=MESH)

    loads = [
        pltpu.make_async_copy(source, target, load_sems.at[k])
        for k, (source, target) in enumerate(
            [(grad_hbm, grad), (first_hbm, old0), (second_hbm, old1), (master_hbm, old2)]
        )
    ]
    for load in loads:
        load.start()

    loads[0].wait()

    def square(n, total):
        block = grad[n // 18, :, pl.ds(pl.multiple_of((n % 18) * CHUNK, CHUNK), CHUNK)].astype(jnp.float32)
        return total + block * block

    squares = lax.fori_loop(0, 54, square, jnp.zeros((16, CHUNK), jnp.float32))
    squares = jnp.sum(squares, axis=0, keepdims=True)
    lanes = squares[:, 0:128] + squares[:, 128:256] + squares[:, 256:384] + squares[:, 384:512]
    pair_rows[shard] = lanes

    for load in loads[1:]:
        load.wait()

    @pl.loop(0, N_DP)
    def _(j):
        base = j * PER_PEER
        rows = [send_ref[base + q] for q in range(PER_PEER)]
        for old, send in zip(olds, sends, strict=True):
            for half in range(2):
                tiles = [old[row + half * (NSEG * 8)] for row in rows]
                for q, tile in enumerate(tiles):
                    send[half * BLOCKS + base + q] = tile

    own = pl.ds(parity * BLOCKS + me * PER_PEER, PER_PEER)
    for send, recv in zip(sends, recvs, strict=True):
        recv[own] = send[own]

    pl.semaphore_wait(barrier, 130)

    for k in (1, 2, 3):
        pltpu.make_async_remote_copy(
            src_ref=pair_rows.at[shard],
            dst_ref=pair_rows.at[shard],
            send_sem=small_send.at[0],
            recv_sem=small_recv.at[0],
            device_id=(me, (shard + k) % 4),
            device_id_type=MESH,
        ).start()

    def send_all(a):
        @pl.loop(0, 127)
        def _(n):
            j, half = peer_of(n)
            pltpu.make_async_remote_copy(
                src_ref=sends[a].at[pl.ds(half * BLOCKS + j * PER_PEER, PER_PEER)],
                dst_ref=recvs[a].at[pl.ds(parity * BLOCKS + me * PER_PEER, PER_PEER)],
                send_sem=send_sem,
                recv_sem=recv_sems.at[a],
                device_id=(j, even_shard + half),
                device_id_type=MESH,
            ).start()

    send_all(0)

    three = pair_rows.at[pl.ds(0, 3)]
    pltpu.make_async_copy(three, three, small_recv.at[0]).wait()
    lanes = pair_rows[0] + pair_rows[1] + pair_rows[2] + pair_rows[3]
    own_row[0] = lanes
    all_rows[me] = lanes

    ids = lax.broadcasted_iota(jnp.int32, (RD, 128), 0) * 128 + lax.broadcasted_iota(jnp.int32, (RD, 128), 1)

    def find(n, table):
        for q in range(16):
            k = n * 16 + q
            table = jnp.where(ids == place_ref[k], k, table)
        return table

    inverse[...] = lax.fori_loop(0, BLOCKS // 16, find, jnp.zeros((RD, 128), jnp.int32))
    table_copy = pltpu.make_async_copy(inverse, inverse_smem, table_sem)
    table_copy.start()

    @pl.loop(0, 63)
    def _(n):
        j, _ = peer_of(jnp.where(n < 32, 32 + n, 64 + n))
        pltpu.make_async_remote_copy(
            src_ref=own_row.at[0],
            dst_ref=all_rows.at[me],
            send_sem=small_send.at[1],
            recv_sem=small_recv.at[1],
            device_id=(j, shard),
            device_id_type=MESH,
        ).start()

    send_all(1)
    send_all(2)
    table_copy.wait()

    def arrive(a):
        span = recvs[a].at[pl.ds(0, 127 * PER_PEER)]
        pltpu.make_async_copy(span, span, recv_sems.at[a]).wait()

        @pl.loop(0, 3 * NSEG)
        def _(n):
            group, s = n // NSEG, n % NSEG
            places = [inverse_smem[group * 16 + r, s] for r in range(16)]
            for half in range(2):
                column = pl.ds(pl.multiple_of(half * HALF + s * 128, 128), 128)
                tiles = [recvs[a][place + half * BLOCKS] for place in places]
                for r, tile in enumerate(tiles):
                    news[a][group, pl.ds(r, 1), column] = tile

    def each_chunk(body):
        @pl.loop(0, 54)
        def _(n):
            body(n // 18, pl.ds(pl.multiple_of((n % 18) * CHUNK, CHUNK), CHUNK))

    arrive(0)
    rest = all_rows.at[pl.ds(0, 63)]
    pltpu.make_async_copy(rest, rest, small_recv.at[1]).wait()
    total = all_rows[0]
    for k in range(1, N_DP):
        total = total + all_rows[k]
    sum_squares = jnp.sum(total, axis=(0, 1), keepdims=True)
    limit = clip_ratio * jnp.sqrt(jnp.float32(ROWS * FF))
    clip_scale = jnp.minimum(1.0, limit / jnp.sqrt(sum_squares + 1e-06))

    def first_step(group, columns):
        scaled = clip_scale * grad[group, :, columns].astype(jnp.float32)
        new0[group, :, columns] = beta_one * new0[group, :, columns] + (1.0 - beta_one) * scaled

    def second_step(group, columns):
        scaled = clip_scale * grad[group, :, columns].astype(jnp.float32)
        moment2 = beta_two * new1[group, :, columns] + (1.0 - beta_two) * scaled * scaled
        new1[group, :, columns] = moment2
        moment1 = new0[group, :, columns]
        update[group, :, columns] = moment1 / correct_one / (jnp.sqrt(moment2 / correct_two) + adam_eps)

    def master_step(group, columns):
        value = new2[group, :, columns]
        new2[group, :, columns] = value - learning_rate * (update[group, :, columns] + weight_decay * value)

    each_chunk(first_step)
    pltpu.make_async_copy(new0, first_out, out_sems.at[0]).start()
    arrive(1)
    each_chunk(second_step)
    pltpu.make_async_copy(new1, second_out, out_sems.at[1]).start()
    arrive(2)
    each_chunk(master_step)
    pltpu.make_async_copy(new2, master_out, out_sems.at[2]).start()

    for send in sends:
        span = send.at[pl.ds(0, 127 * PER_PEER)]
        pltpu.make_async_copy(span, span, send_sem).wait()
    pltpu.make_async_copy(three, three, small_send.at[0]).wait()
    pltpu.make_async_copy(rest, rest, small_send.at[1]).wait()
    for a in range(3):
        pltpu.make_async_copy(news[a], outs[a], out_sems.at[a]).wait()


def per_device(master_old, moment1_old, moment2_old, grad, send_slots, recv_slots):
    def rows_of(matrix):
        return matrix.reshape(RD // 8, 8, COLS // 128, 128).transpose(0, 2, 1, 3).reshape(TILES, 1, 128)

    slot = send_slots[0]
    row, segment = slot // NSEG, slot % NSEG
    send_rows = ((row // 8) * (COLS // 128) + segment) * 8 + row % 8
    slot = recv_slots[0]
    place = (slot // NSEG) * 128 + slot % NSEG
    smem = pl.BlockSpec(memory_space=pltpu.SMEM)
    hbm = pl.BlockSpec(memory_space=pl.ANY)
    tiles = pltpu.VMEM((TILES, 1, 128), jnp.float32)
    whole = pltpu.VMEM((3, 16, COLS), jnp.float32)
    new = pl.pallas_call(
        kernel,
        out_shape=[jax.ShapeDtypeStruct((3, 16, COLS), jnp.float32)] * 3,
        in_specs=[smem, smem, hbm, hbm, hbm, hbm],
        out_specs=[hbm, hbm, hbm],
        scratch_shapes=[tiles] * 9
        + [whole] * 3
        + [
            pltpu.VMEM((3, 16, COLS), jnp.bfloat16),
            whole,
            pltpu.VMEM((4, 1, 128), jnp.float32),
            pltpu.VMEM((1, 1, 128), jnp.float32),
            pltpu.VMEM((N_DP, 1, 128), jnp.float32),
            pltpu.VMEM((RD, 128), jnp.int32),
            pltpu.SMEM((RD, 128), jnp.int32),
            pltpu.SemaphoreType.DMA((4,)),
            pltpu.SemaphoreType.DMA((3,)),
            pltpu.SemaphoreType.DMA,
            pltpu.SemaphoreType.DMA((3,)),
            pltpu.SemaphoreType.DMA((2,)),
            pltpu.SemaphoreType.DMA((2,)),
            pltpu.SemaphoreType.DMA,
        ],
        compiler_params=pltpu.CompilerParams(
            collective_id=0, has_side_effects=True, vmem_limit_bytes=56 * 2**20
        ),
    )(send_rows, place, rows_of(moment1_old), rows_of(moment2_old), rows_of(master_old), grad.reshape(3, 16, COLS))
    moment1, moment2, master = [array.reshape(RD, COLS) for array in new]
    return (master, moment1, moment2)


def solution(mesh):
    specs = (P("dp", "tensor"),) * 4 + (P("dp", None),) * 2
    return jax.shard_map(
        per_device, mesh=mesh, in_specs=specs, out_specs=(P("dp", "tensor"),) * 3, check_vma=False
    )
```

time: 304 us -> 156 us (0.51); the launches traced: 299 us -> 155 us
  Pallas kernels: 0 us -> 144 us
  waiting for transfers between devices: 109 us -> 0 us
  local copies, waits for them, and re-layouts: 81.9 us -> 6.25 us
  blocking collectives: 58.8 us -> 0 us
  other arithmetic: 33 us -> 3.6 us
  starting transfers between devices: 14.7 us -> 0 us
    pallas_call x0 -> x1, Pallas kernels: none -> 144 us  [per_device(): pl.pallas_call(kernel, out_shape=[jax.ShapeDtypeStruct((3, 16, COLS), jnp...]
    all_to_all x1 -> x0, waiting for transfers between devices: 109 us -> none  [per_device(): lax.all_to_all(outgoing, DP, split_axis=1, concat_axis=1, tiled=True)]
    psum x4 -> x0, blocking collectives: 58.8 us -> none  [one_axis_at_a_time(): return functools.reduce(lax.psum, axes, value)]
    gather x2 -> x0, local copies, waits for them, and re-layouts: 30.7 us -> none  [the longest x1 15.4 us: per_device(): tiles = jnp.take(arrived, inverse, axis=1)]
    select_n x6 -> x0, other arithmetic: 20.1 us -> none  [the longest x2 8.07 us: per_device(): jnp.take(tiled, own_send, axis=1).reshape(3, devices, per_peer, 2, SEGW)]
    all_to_all x1 -> x0, starting transfers between devices: 13.5 us -> none  [per_device(): lax.all_to_all(outgoing, DP, split_axis=1, concat_axis=1, tiled=True)]
    another operation x6 -> x0, local copies, waits for them, and re-layouts: 11.8 us -> none  [the longest x3 7.1 us: per_device(): stacked = jnp.stack([master_old, moment1_old, moment2_old], 0)]
    scatter x1 -> x0, local copies, waits for them, and re-layouts: 8.77 us -> none  [per_device(): jnp.zeros((blocks,), jnp.int32).at[own_recv]]
  transfers between devices with their start and end apart: 2 -> 0, of which waited for: 1 -> 0; matrix products, arithmetic and copies ran while one was open for 5% -> 0% of each run, Pallas kernels for 0% -> 0%
where the time goes in v1:
time: 156 us; the launch traced here: 155 us
  Pallas kernels  144 us (92%)
  local copies, waits for them, and re-layouts  6.25 us (4%)
  other arithmetic  3.6 us (2%)
    pallas_call x1, Pallas kernels, per_device(): pl.pallas_call(kernel, out_shape=[jax.ShapeDtypeStruct((3, 16, COLS), jnp...  144 us
    unnamed x7, local copies, waits for them, and re-layouts  6.25 us

profile of v1, /device:TPU:1, one launch (start us, length us, event | category | flops | bytes accessed | tf_op | source)
XLA Modules:
  0.0 154.7 jit_solution(3856290513428754106)
XLA Ops:
  0.6 0.7 compare_reduce_fusion.1
  1.4 0.7 compare_reduce_fusion
  2.1 0.8 divide_reduce_fusion.1
  2.9 0.8 remainder_reduce_fusion
  3.6 0.6 fusion.3
  4.2 144.1 %shard_map.85 = (f32[3,16,9216]{2,1,0:T(8,128)}, f32[3,16,9216]{2,1,0:T(8,128)}, f32[3,16,9216]{2,1,0:T(8,128)}) custom-call(s32[1728]{0:T(1024)} %get-tuple-element.13.send_ref, s32[1728]{0:T(1024)} %get-tuple-element.14.place_ref, f32[3456,1,128]{2,1,0:T(1,128)} %bitcast.19, f32[3456,1,128]{2,1,0:T(1,128)} %bitcast.20, f32[3456,1,128]{2,1,0:T(1,128)} %bitcast.21, ...), custom_call_target="tpu_custom_call" | custom-call | tf_op jit(solution)/shard_map/pallas_call | solution.py:244
  148.4 0.0 copy-start.1
  148.4 2.9 %copy.12 = f32[48,9216]{1,0:T(8,128)} copy(f32[48,9216]{1,0:T(8,128)} %bitcast.24) | data formatting | bytes 3538944
  151.3 0.0 copy-done.1
  151.3 0.0 copy-start
  151.3 1.2 copy.13
  152.5 0.9 copy-done
  153.4 1.2 copy.14
Async XLA Ops:
  148.4 2.9 %copy-start.1 = (f32[3,16,9216]{2,1,0:T(8,128)S(1)}, f32[3,16,9216]{2,1,0:T(8,128)}, u32[]{:S(2)}) copy-start(f32[3,16,9216]{2,1,0:T(8,128)} %get-tuple-element.7) | copy-start | bytes 5308420
  151.3 2.1 %copy-start = (f32[3,16,9216]{2,1,0:T(8,128)S(1)}, f32[3,16,9216]{2,1,0:T(8,128)}, u32[]{:S(2)}) copy-start(f32[3,16,9216]{2,1,0:T(8,128)} %get-tuple-element.8) | copy-start | bytes 5308420

commit v2 on v1

v2 whole, which is shorter than its diff:
```python
import functools

import jax
import jax.numpy as jnp
from jax import lax
from jax.experimental import pallas as pl
from jax.experimental.pallas import tpu as pltpu
from jax.sharding import PartitionSpec as P

ROWS = 3072
FF = 36864
SEGW = 128
RD = 48
COLS = 9216
HALF = 4608
NSEG = 36
BLOCKS = 1728
N_DP = 64
PER_PEER = 27
TILES = 2 * BLOCKS
MESH = pl.DeviceIdType.MESH

beta_one = 0.9
beta_two = 0.95
correct_one = 0.6513215599
correct_two = 0.4012630608
adam_eps = 1e-08
learning_rate = 0.01
weight_decay = 0.1
clip_ratio = 0.75

CHUNK = 512


def kernel(
    send_hbm, place_hbm, first_hbm, second_hbm, master_hbm, grad_hbm,
    new0, new1, new2, update,
    old0, old1, old2, send0, send1, send2, recv0, recv1, recv2,
    grad, pair_rows, own_row, all_rows, slots, source_rows, inverse, send_ref, place_ref, inverse_smem,
    load_sems, table_sems, send_sem, recv_sems, small_send, small_recv, entered,
):
    me = lax.axis_index("dp")
    shard = lax.axis_index("tensor")
    z, x, core = me // 8, (me // 2) % 4, me % 2
    parity = shard % 2
    partner = shard + 1 - 2 * parity
    olds, sends, recvs, news = (old0, old1, old2), (send0, send1, send2), (recv0, recv1, recv2), (new0, new1, new2)

    def dp_at(dz, dx, dc):
        return (((z + dz) % 8) * 4 + (x + dx) % 4) * 2 + (core + dc) % 2

    def signal(semaphore, j, t):
        pl.semaphore_signal(semaphore, inc=1, device_id=(j, t), device_id_type=MESH)

    barrier = pltpu.get_barrier_semaphore()
    for k in (4, 3, 5, 2, 6, 1, 7):
        signal(barrier, dp_at(k, 0, 0), shard)
    for k in (2, 1, 3):
        signal(barrier, dp_at(0, k, 0), shard)
    signal(barrier, dp_at(0, 0, 1), shard)
    for k in (1, 2, 3):
        signal(barrier, me, (shard + k) % 4)

    loads = [
        pltpu.make_async_copy(source, target, load_sems.at[k])
        for k, (source, target) in enumerate(
            [
                (send_hbm, slots),
                (first_hbm, old0),
                (second_hbm, old1),
                (master_hbm, old2),
                (grad_hbm, grad),
                (place_hbm, place_ref),
            ]
        )
    ]
    for load in loads:
        load.start()

    loads[0].wait()
    slot = slots[...]
    row = (slot * 1821) >> 16
    source_rows[...] = slot * 8 + (row >> 3) * (COLS // 128 * 8) - row * (NSEG * 8) + (row & 7)
    rows_copy = pltpu.make_async_copy(source_rows, send_ref, table_sems.at[0])
    rows_copy.start()
    for load in loads[1:5]:
        load.wait()

    def square(n, total):
        block = grad[n // 18, :, pl.ds(pl.multiple_of((n % 18) * CHUNK, CHUNK), CHUNK)].astype(jnp.float32)
        return total + block * block

    squares = lax.fori_loop(0, 54, square, jnp.zeros((16, CHUNK), jnp.float32))
    squares = jnp.sum(squares, axis=0, keepdims=True)
    pair_rows[shard] = squares[:, 0:128] + squares[:, 128:256] + squares[:, 256:384] + squares[:, 384:512]
    rows_copy.wait()

    def along_z(k):
        return jnp.where(k % 2 == 0, 4 + k // 2, 3 - k // 2)

    def offset_of(n):
        plane, other = n - 11, n - 32
        dz = jnp.where(n < 7, along_z(n), jnp.where(n < 11, 0, jnp.where(n < 32, along_z(plane % 7), along_z(other % 8))))
        dx = jnp.where(n < 7, 0, jnp.where(n < 11, (n - 6) % 4, jnp.where(n < 32, 1 + plane // 7, (other // 8 + 1) % 4)))
        dc = jnp.where(n == 10, 1, jnp.where(n < 32, 0, 1))
        return dp_at(dz % 8, dx, jnp.where(n == 63, 0, dc))

    def gather(n):
        base = offset_of(n) * PER_PEER
        rows = [send_ref[0, base + q] for q in range(PER_PEER)]
        for old, send in zip(olds, sends, strict=True):
            for half in range(2):
                tiles = [old[row + half * (NSEG * 8)] for row in rows]
                for q, tile in enumerate(tiles):
                    send[half * BLOCKS + base + q] = tile

    def deliver(a, j, t, half):
        pltpu.make_async_remote_copy(
            src_ref=sends[a].at[pl.ds(half * BLOCKS + j * PER_PEER, PER_PEER)],
            dst_ref=recvs[a].at[pl.ds(parity * BLOCKS + me * PER_PEER, PER_PEER)],
            send_sem=send_sem,
            recv_sem=recv_sems.at[a],
            device_id=(j, t),
            device_id_type=MESH,
        ).start()

    def deliver_here(a, n):
        deliver(a, offset_of(n), shard, parity)

    def deliver_partner(a, n):
        deliver(a, offset_of(n), partner, 1 - parity)

    def gather_and_deliver(first, last):
        @pl.loop(first, last)
        def _(n):
            gather(n)
            deliver_here(0, n - 1)

    EARLY = 4

    @pl.loop(0, EARLY)
    def _(n):
        gather(n)

    pl.semaphore_wait(barrier, 14)
    for k in (2, 1, 3):
        signal(entered.at[0], dp_at(0, k, 0), shard)
    for k in (1, 2, 3):
        pltpu.make_async_remote_copy(
            src_ref=pair_rows.at[shard],
            dst_ref=pair_rows.at[shard],
            send_sem=small_send.at[0],
            recv_sem=small_recv.at[0],
            device_id=(me, (shard + k) % 4),
            device_id_type=MESH,
        ).start()

    @pl.loop(0, EARLY - 1)
    def _(n):
        deliver_here(0, n)

    gather_and_deliver(EARLY, 12)
    pl.semaphore_wait(entered.at[0], 3)
    signal(entered.at[1], dp_at(0, 0, 1), shard)
    gather_and_deliver(12, 33)
    pl.semaphore_wait(entered.at[1], 1)
    signal(entered.at[2], me, partner)
    gather_and_deliver(33, 64)
    pl.semaphore_wait(entered.at[2], 1)

    @pl.loop(0, 64)
    def _(n):
        deliver_partner(0, n)

    own = pl.ds(parity * BLOCKS + me * PER_PEER, PER_PEER)
    for send, recv in zip(sends, recvs, strict=True):
        recv[own] = send[own]

    three = pair_rows.at[pl.ds(0, 3)]
    pltpu.make_async_copy(three, three, small_recv.at[0]).wait()
    lanes = pair_rows[0] + pair_rows[1] + pair_rows[2] + pair_rows[3]
    own_row[0] = lanes
    all_rows[me] = lanes

    loads[5].wait()
    lane = lax.broadcasted_iota(jnp.int32, (RD, 128), 1)
    ids = jnp.where(lane < NSEG, lax.broadcasted_iota(jnp.int32, (RD, 128), 0) * NSEG + lane, -1)

    def find(n, table):
        for q in range(16):
            k = n * 16 + q
            table = jnp.where(ids == place_ref[0, k], k, table)
        return table

    inverse[...] = lax.fori_loop(0, BLOCKS // 16, find, jnp.zeros((RD, 128), jnp.int32))
    table_copy = pltpu.make_async_copy(inverse, inverse_smem, table_sems.at[1])
    table_copy.start()

    @pl.loop(0, 63)
    def _(n):
        pltpu.make_async_remote_copy(
            src_ref=own_row.at[0],
            dst_ref=all_rows.at[me],
            send_sem=small_send.at[1],
            recv_sem=small_recv.at[1],
            device_id=(offset_of(n), shard),
            device_id_type=MESH,
        ).start()

    for a in (1, 2):

        @pl.loop(0, 63)
        def _(n):
            deliver_here(a, n)

        @pl.loop(0, 64)
        def _(n):
            deliver_partner(a, n)

    table_copy.wait()

    def arrive(a):
        span = recvs[a].at[pl.ds(0, 127 * PER_PEER)]
        pltpu.make_async_copy(span, span, recv_sems.at[a]).wait()

        @pl.loop(0, 3 * NSEG)
        def _(n):
            group, s = n // NSEG, n % NSEG
            places = [inverse_smem[group * 16 + r, s] for r in range(16)]
            for half in range(2):
                column = pl.ds(pl.multiple_of(half * HALF + s * 128, 128), 128)
                tiles = [recvs[a][place + half * BLOCKS] for place in places]
                for r, tile in enumerate(tiles):
                    news[a][group, pl.ds(r, 1), column] = tile

    def each_chunk(body):
        @pl.loop(0, 54)
        def _(n):
            body(n // 18, pl.ds(pl.multiple_of((n % 18) * CHUNK, CHUNK), CHUNK))

    arrive(0)
    rest = all_rows.at[pl.ds(0, 63)]
    pltpu.make_async_copy(rest, rest, small_recv.at[1]).wait()
    total = all_rows[0]
    for k in range(1, N_DP):
        total = total + all_rows[k]
    sum_squares = jnp.sum(total, axis=(0, 1), keepdims=True)
    limit = clip_ratio * jnp.sqrt(jnp.float32(ROWS * FF))
    clip_scale = jnp.minimum(1.0, limit / jnp.sqrt(sum_squares + 1e-06))

    def first_step(group, columns):
        scaled = clip_scale * grad[group, :, columns].astype(jnp.float32)
        new0[group, :, columns] = beta_one * new0[group, :, columns] + (1.0 - beta_one) * scaled

    def second_step(group, columns):
        scaled = clip_scale * grad[group, :, columns].astype(jnp.float32)
        moment2 = beta_two * new1[group, :, columns] + (1.0 - beta_two) * scaled * scaled
        new1[group, :, columns] = moment2
        moment1 = new0[group, :, columns]
        update[group, :, columns] = moment1 / correct_one / (jnp.sqrt(moment2 / correct_two) + adam_eps)

    each_chunk(first_step)
    arrive(1)
    each_chunk(second_step)
    for send in sends[:2]:
        span = send.at[pl.ds(0, 127 * PER_PEER)]
        pltpu.make_async_copy(span, span, send_sem).wait()
    pltpu.make_async_copy(three, three, small_send.at[0]).wait()
    pltpu.make_async_copy(rest, rest, small_send.at[1]).wait()
    arrive(2)
    span = send2.at[pl.ds(0, 127 * PER_PEER)]
    pltpu.make_async_copy(span, span, send_sem).wait()


def finish(new0, new1, new2, update, first_out, second_out, master_out, master, sems):
    copies = [
        pltpu.make_async_copy(new0, first_out, sems.at[0]),
        pltpu.make_async_copy(new1, second_out, sems.at[1]),
    ]
    for copy in copies:
        copy.start()
    for group in range(3):

        @pl.loop(0, COLS // CHUNK)
        def _(n):
            columns = pl.ds(pl.multiple_of(n * CHUNK, CHUNK), CHUNK)
            value = new2[group, :, columns]
            master[group, :, columns] = value - learning_rate * (update[group, :, columns] + weight_decay * value)

        copy = pltpu.make_async_copy(master.at[group], master_out.at[group], sems.at[2 + group])
        copy.start()
        copies.append(copy)
    for copy in copies:
        copy.wait()


def per_device(master_old, moment1_old, moment2_old, grad, send_slots, recv_slots):
    def rows_of(matrix):
        return matrix.reshape(RD // 8, 8, COLS // 128, 128).transpose(0, 2, 1, 3).reshape(TILES, 1, 128)

    hbm = pl.BlockSpec(memory_space=pl.ANY)
    tiles = pltpu.VMEM((TILES, 1, 128), jnp.float32)
    whole = pltpu.VMEM((3, 16, COLS), jnp.float32)
    vmem = pl.BlockSpec(memory_space=pltpu.VMEM)
    kept = pl.pallas_call(
        kernel,
        out_shape=[pltpu.VMEM((3, 16, COLS), jnp.float32)] * 4,
        in_specs=[hbm] * 6,
        out_specs=[vmem] * 4,
        scratch_shapes=[tiles] * 9
        + [
            pltpu.VMEM((3, 16, COLS), jnp.bfloat16),
            pltpu.VMEM((4, 1, 128), jnp.float32),
            pltpu.VMEM((1, 1, 128), jnp.float32),
            pltpu.VMEM((N_DP, 1, 128), jnp.float32),
            pltpu.VMEM((1, BLOCKS), jnp.int32),
            pltpu.VMEM((1, BLOCKS), jnp.int32),
            pltpu.VMEM((RD, 128), jnp.int32),
            pltpu.SMEM((1, BLOCKS), jnp.int32),
            pltpu.SMEM((1, BLOCKS), jnp.int32),
            pltpu.SMEM((RD, 128), jnp.int32),
            pltpu.SemaphoreType.DMA((6,)),
            pltpu.SemaphoreType.DMA((2,)),
            pltpu.SemaphoreType.DMA,
            pltpu.SemaphoreType.DMA((3,)),
            pltpu.SemaphoreType.DMA((2,)),
            pltpu.SemaphoreType.DMA((2,)),
            pltpu.SemaphoreType.REGULAR((3,)),
        ],
        compiler_params=pltpu.CompilerParams(
            collective_id=0, has_side_effects=True, vmem_limit_bytes=57 * 2**20
        ),
    )(send_slots, recv_slots, rows_of(moment1_old), rows_of(moment2_old), rows_of(master_old), grad.reshape(3, 16, COLS))
    new = pl.pallas_call(
        finish,
        out_shape=[jax.ShapeDtypeStruct((3, 16, COLS), jnp.float32)] * 3,
        in_specs=[vmem] * 4,
        out_specs=[hbm] * 3,
        scratch_shapes=[pltpu.VMEM((3, 16, COLS), jnp.float32), pltpu.SemaphoreType.DMA((5,))],
        compiler_params=pltpu.CompilerParams(vmem_limit_bytes=16 * 2**20),
    )(*kept)
    moment1, moment2, master = [array.reshape(RD, COLS) for array in new]
    return (master, moment1, moment2)


def solution(mesh):
    specs = (P("dp", "tensor"),) * 4 + (P("dp", None),) * 2
    return jax.shard_map(
        per_device, mesh=mesh, in_specs=specs, out_specs=(P("dp", "tensor"),) * 3, check_vma=False
    )
```

time: 156 us -> 137 us (0.88); the launches traced: 155 us -> 137 us
  Pallas kernels: 144 us -> 137 us
  local copies, waits for them, and re-layouts: 6.25 us -> 0 us
  other arithmetic: 3.6 us -> 0 us
    pallas_call x1 -> x2, Pallas kernels: 144 us -> 137 us  [the longest x1 134 us: per_device(): pl.pallas_call(kernel, out_shape=[pltpu.VMEM((3, 16, COLS), jnp.float32)]...]
    unnamed x7 -> x0, local copies, waits for them, and re-layouts: 6.25 us -> none
where the time goes in v2:
time: 137 us
  Pallas kernels  137 us (100%)
    pallas_call x1, Pallas kernels, per_device(): pl.pallas_call(kernel, out_shape=[pltpu.VMEM((3, 16, COLS), jnp.float32)]...  134 us

profile of v2, /device:TPU:1, one launch (start us, length us, event | category | flops | bytes accessed | tf_op | source)
XLA Modules:
  0.0 137.3 jit_solution(3515021212652498198)
XLA Ops:
  0.6 134.3 %shard_map.85 = (f32[3,16,9216]{2,1,0:T(8,128)S(1)}, f32[3,16,9216]{2,1,0:T(8,128)S(1)}, f32[3,16,9216]{2,1,0:T(8,128)S(1)}, f32[3,16,9216]{2,1,0:T(8,128)S(1)}) custom-call(s32[1,1728]{1,0:T(1,128)} %send_hbm.1, s32[1,1728]{1,0:T(1,128)} %place_hbm.1, f32[3456,1,128]{2,1,0:T(1,128)} %bitcast.19, f32[3456,1,128]{2,1,0:T(1,128)} %bitcast.20, ...), custom_call_target="tpu_custom_call" | custom-call | tf_op jit(solution)/shard_map/pallas_call | solution.py:305
  134.9 2.4 %shard_map.86 = (f32[3,16,9216]{2,1,0:T(8,128)}, f32[3,16,9216]{2,1,0:T(8,128)}, f32[3,16,9216]{2,1,0:T(8,128)}) custom-call(f32[3,16,9216]{2,1,0:T(8,128)S(1)} %get-tuple-element.10.new0, f32[3,16,9216]{2,1,0:T(8,128)S(1)} %get-tuple-element.11.new1, f32[3,16,9216]{2,1,0:T(8,128)S(1)} %get-tuple-element.12.new2, f32[3,16,9216]{2,1,0:T(8,128)S(1)} %get-tuple-element.13.update), custom_call_target="tpu_custom_call" | custom-call | tf_op jit(solution)/shard_map/pallas_call | solution.py:334

commit v3 on v2

v3 whole, which is shorter than its diff:
```python
import functools

import jax
import jax.numpy as jnp
from jax import lax
from jax.experimental import pallas as pl
from jax.experimental.pallas import tpu as pltpu
from jax.sharding import PartitionSpec as P

ROWS = 3072
FF = 36864
SEGW = 128
RD = 48
COLS = 9216
HALF = 4608
NSEG = 36
BLOCKS = 1728
N_DP = 64
PER_PEER = 27
TILES = 2 * BLOCKS
MESH = pl.DeviceIdType.MESH

beta_one = 0.9
beta_two = 0.95
correct_one = 0.6513215599
correct_two = 0.4012630608
adam_eps = 1e-08
learning_rate = 0.01
weight_decay = 0.1
clip_ratio = 0.75

CHUNK = 512
EARLY = 3


def kernel(
    send_hbm, place_hbm, first_hbm, second_hbm, master_hbm, grad_hbm,
    new0, new1, update, recv2, inverse,
    old0, old1, old2, send0, send1, send2, recv0, recv1,
    grad, shard_rows, line_rows, plane_rows, slots, source_rows, send_ref, place_ref, inverse_smem,
    load_sems, table_sems, send_sem, recv_sems, small_send, small_recv, entered,
):
    me = lax.axis_index("dp")
    shard = lax.axis_index("tensor")
    z, x, core = me // 8, (me // 2) % 4, me % 2
    parity = shard % 2
    partner = shard + 1 - 2 * parity
    olds, sends, recvs = (old0, old1, old2), (send0, send1, send2), (recv0, recv1, recv2)

    def dp_at(dz, dx, dc):
        return (((z + dz) % 8) * 4 + (x + dx) % 4) * 2 + (core + dc) % 2

    def signal(semaphore, j, t):
        pl.semaphore_signal(semaphore, inc=1, device_id=(j, t), device_id_type=MESH)

    barrier = pltpu.get_barrier_semaphore()
    for k in (4, 3, 5, 2, 6, 1, 7):
        signal(barrier, dp_at(k, 0, 0), shard)
    for k in (2, 1, 3):
        signal(barrier, dp_at(0, k, 0), shard)
    signal(barrier, dp_at(0, 0, 1), shard)
    for k in (1, 2, 3):
        signal(barrier, me, (shard + k) % 4)

    loads = [
        pltpu.make_async_copy(source, target, load_sems.at[k])
        for k, (source, target) in enumerate(
            [
                (send_hbm, slots),
                (first_hbm, old0),
                (second_hbm, old1),
                (master_hbm, old2),
                (grad_hbm, grad),
                (place_hbm, place_ref),
            ]
        )
    ]
    for load in loads:
        load.start()

    loads[0].wait()
    slot = slots[...]
    row = (slot * 1821) >> 16
    source_rows[...] = slot * 8 + (row >> 3) * (COLS // 128 * 8) - row * (NSEG * 8) + (row & 7)
    rows_copy = pltpu.make_async_copy(source_rows, send_ref, table_sems.at[0])
    rows_copy.start()

    def offset_of(n):
        zi = n & 7
        dz = jnp.where((zi & 1) == 0, 4 + (zi >> 1), 3 - (zi >> 1))
        return (((z + dz) & 7) << 3) + (((x + (n >> 3)) & 3) << 1) + ((core + (n >> 5)) & 1)

    def gather(a, n):
        base = offset_of(n) * PER_PEER
        rows = [send_ref[0, base + q] for q in range(PER_PEER)]
        for half in range(2):
            tiles = [olds[a][row + half * (NSEG * 8)] for row in rows]
            for q, tile in enumerate(tiles):
                sends[a][half * BLOCKS + base + q] = tile

    def deliver(a, j, t, half):
        pltpu.make_async_remote_copy(
            src_ref=sends[a].at[pl.ds(half * BLOCKS + j * PER_PEER, PER_PEER)],
            dst_ref=recvs[a].at[pl.ds(parity * BLOCKS + me * PER_PEER, PER_PEER)],
            send_sem=send_sem,
            recv_sem=recv_sems.at[a],
            device_id=(j, t),
            device_id_type=MESH,
        ).start()

    def deliver_here(a, n):
        deliver(a, offset_of(n), shard, parity)

    def deliver_partner(a, n):
        deliver(a, offset_of(n), partner, 1 - parity)

    def gather_and_deliver(first, last):
        @pl.loop(first, last)
        def _(n):
            gather(0, n)
            deliver_here(0, n - 1)

    rows_copy.wait()
    loads[1].wait()

    @pl.loop(0, EARLY)
    def _(n):
        gather(0, n)

    pl.semaphore_wait(barrier, 14)
    for k in (2, 1, 3):
        signal(entered.at[0], dp_at(0, k, 0), shard)

    @pl.loop(0, EARLY - 1)
    def _(n):
        deliver_here(0, n)

    gather_and_deliver(EARLY, 8)
    gather(0, 8)
    pl.semaphore_wait(entered.at[0], 3)
    signal(entered.at[1], dp_at(0, 0, 1), shard)
    gather_and_deliver(9, 33)
    pl.semaphore_wait(entered.at[1], 1)
    signal(entered.at[2], me, partner)
    gather_and_deliver(33, 64)
    pl.semaphore_wait(entered.at[2], 1)

    @pl.loop(0, 64)
    def _(n):
        deliver_partner(0, n)

    deliver_here(0, 63)

    loads[4].wait()

    def square(n, total):
        group = jnp.where(n >= 18, 1, 0) + jnp.where(n >= 36, 1, 0)
        columns = pl.ds(pl.multiple_of((n - 18 * group) * CHUNK, CHUNK), CHUNK)
        block = grad[group, :, columns].astype(jnp.float32)
        return total + block * block

    squares = lax.fori_loop(0, 54, square, jnp.zeros((16, CHUNK), jnp.float32))
    squares = jnp.sum(squares, axis=0, keepdims=True)
    shard_rows[shard] = squares[:, 0:128] + squares[:, 128:256] + squares[:, 256:384] + squares[:, 384:512]

    def pass_row(k, rows, own, j, t):
        pltpu.make_async_remote_copy(
            src_ref=rows.at[own],
            dst_ref=rows.at[own],
            send_sem=small_send.at[k],
            recv_sem=small_recv.at[k],
            device_id=(j, t),
            device_id_type=MESH,
        ).start()

    def wait_rows(rows, semaphore):
        others = rows.at[pl.ds(0, rows.shape[0] - 1)]
        pltpu.make_async_copy(others, others, semaphore).wait()

    def sum_of(rows):
        total = rows[0]
        for k in range(1, rows.shape[0]):
            total = total + rows[k]
        return total

    def gather_all(a):
        @pl.loop(0, 64)
        def _(n):
            gather(a, n)

        own = pl.ds(parity * BLOCKS + me * PER_PEER, PER_PEER)
        recvs[a][own] = sends[a][own]

    def deliver_all(a):
        def peer(n):
            zi, xi = n & 7, (n >> 3) & 3
            dz = jnp.where((zi & 1) == 0, 4 + (zi >> 1), 3 - (zi >> 1))
            dx = jnp.where(xi == 0, 2, jnp.where(xi == 3, 0, 2 * xi - 1))
            return (((z + dz) & 7) << 3) + (((x + dx) & 3) << 1) + ((core + 1 - (n >> 5)) & 1)

        @pl.loop(0, 63)
        def _(n):
            deliver(a, peer(n), shard, parity)
            deliver(a, peer(n), partner, 1 - parity)

        deliver(a, me, partner, 1 - parity)

    own = pl.ds(parity * BLOCKS + me * PER_PEER, PER_PEER)
    recv0[own] = send0[own]
    loads[2].wait()
    gather_all(1)
    for k in (1, 2, 3):
        pass_row(0, shard_rows, shard, me, (shard + k) % 4)
    loads[3].wait()
    gather_all(2)
    wait_rows(shard_rows, small_recv.at[0])
    line_rows[z * 2 + core] = sum_of(shard_rows)

    loads[5].wait()
    line = lax.broadcasted_iota(jnp.int32, (16, 128), 0)
    lane = lax.broadcasted_iota(jnp.int32, (16, 128), 1)
    group = jnp.where(line >= 5, 1, 0) + jnp.where(line >= 10, 1, 0)
    segment = (line - 5 * group) * 8 + (lane >> 4)
    ids = jnp.where((segment < NSEG) & (line < 15), (group * 16 + (lane & 15)) * NSEG + segment, -1)

    def find(n, table):
        for q in range(16):
            k = n * 16 + q
            table = jnp.where(ids == place_ref[0, k], k, table)
        return table

    inverse[...] = lax.fori_loop(0, BLOCKS // 16, find, jnp.zeros((16, 128), jnp.int32))
    table_copy = pltpu.make_async_copy(inverse, inverse_smem, table_sems.at[1])
    table_copy.start()

    for k in range(1, 16):
        pass_row(1, line_rows, z * 2 + core, dp_at(k >> 1, 0, k & 1), shard)
    deliver_all(1)
    table_copy.wait()

    def arrive(a, new):
        span = recvs[a].at[pl.ds(0, 127 * PER_PEER)]
        pltpu.make_async_copy(span, span, recv_sems.at[a]).wait()

        @pl.loop(0, 12)
        def _(n):
            place(recvs[a], inverse_smem, new, (n >> 2) * 5 + (n & 3), n >> 2, (n & 3) * 8, 8)

        @pl.loop(0, 3)
        def _(n):
            place(recvs[a], inverse_smem, new, n * 5 + 4, n, 32, 4)

    def each_chunk(body):
        @pl.loop(0, 54)
        def _(n):
            group = jnp.where(n >= 18, 1, 0) + jnp.where(n >= 36, 1, 0)
            body(group, pl.ds(pl.multiple_of((n - 18 * group) * CHUNK, CHUNK), CHUNK))

    wait_rows(line_rows, small_recv.at[1])
    plane_rows[x] = sum_of(line_rows)
    arrive(0, new0)
    for k in (1, 2, 3):
        pass_row(2, plane_rows, x, dp_at(0, k, 0), shard)
    deliver_all(2)
    arrive(1, new1)

    wait_rows(plane_rows, small_recv.at[2])
    total = sum_of(plane_rows)
    sum_squares = jnp.sum(total, axis=(0, 1), keepdims=True)
    limit = clip_ratio * jnp.sqrt(jnp.float32(ROWS * FF))
    clip_scale = jnp.minimum(1.0, limit / jnp.sqrt(sum_squares + 1e-06))

    def first_step(group, columns):
        scaled = clip_scale * grad[group, :, columns].astype(jnp.float32)
        new0[group, :, columns] = beta_one * new0[group, :, columns] + (1.0 - beta_one) * scaled

    def second_step(group, columns):
        scaled = clip_scale * grad[group, :, columns].astype(jnp.float32)
        moment2 = beta_two * new1[group, :, columns] + (1.0 - beta_two) * scaled * scaled
        new1[group, :, columns] = moment2
        moment1 = new0[group, :, columns]
        update[group, :, columns] = moment1 / correct_one / (jnp.sqrt(moment2 / correct_two) + adam_eps)

    each_chunk(first_step)
    each_chunk(second_step)
    for rows, semaphore in zip((shard_rows, line_rows, plane_rows), range(3), strict=True):
        wait_rows(rows, small_send.at[semaphore])
    for a in range(3):
        span = sends[a].at[pl.ds(0, 127 * PER_PEER)]
        pltpu.make_async_copy(span, span, send_sem).wait()
    span = recv2.at[pl.ds(0, 127 * PER_PEER)]
    pltpu.make_async_copy(span, span, recv_sems.at[2]).wait()


def place(recv, inverse, new, line, group, segment, count):
    for u in range(count):
        tiles = []
        for r in range(16):
            source = inverse[line, u * 16 + r]
            tiles.append((recv[source], recv[source + BLOCKS]))
        for half in range(2):
            column = pl.ds(pl.multiple_of((half * NSEG + segment + u) * 128, 128), 128)
            for r in range(16):
                new[group, pl.ds(r, 1), column] = tiles[r][half]


def finish(new0, new1, update, recv2, inverse, first_out, second_out, master_out, master, inverse_smem, sems):
    table = pltpu.make_async_copy(inverse, inverse_smem, sems.at[5])
    table.start()
    copies = [
        pltpu.make_async_copy(new0, first_out, sems.at[0]),
        pltpu.make_async_copy(new1, second_out, sems.at[1]),
    ]
    for copy in copies:
        copy.start()
    table.wait()
    for group in range(3):

        @pl.loop(0, 4)
        def _(n):
            place(recv2, inverse_smem, master, group * 5 + n, group, n * 8, 8)

        place(recv2, inverse_smem, master, group * 5 + 4, group, 32, 4)

        @pl.loop(0, COLS // CHUNK)
        def _(n):
            columns = pl.ds(pl.multiple_of(n * CHUNK, CHUNK), CHUNK)
            value = master[group, :, columns]
            master[group, :, columns] = value - learning_rate * (update[group, :, columns] + weight_decay * value)

        copy = pltpu.make_async_copy(master.at[group], master_out.at[group], sems.at[2 + group])
        copy.start()
        copies.append(copy)
    for copy in copies:
        copy.wait()


def per_device(master_old, moment1_old, moment2_old, grad, send_slots, recv_slots):
    def rows_of(matrix):
        return matrix.reshape(RD // 8, 8, COLS // 128, 128).transpose(0, 2, 1, 3).reshape(TILES, 1, 128)

    hbm = pl.BlockSpec(memory_space=pl.ANY)
    tiles = pltpu.VMEM((TILES, 1, 128), jnp.float32)
    whole = pltpu.VMEM((3, 16, COLS), jnp.float32)
    vmem = pl.BlockSpec(memory_space=pltpu.VMEM)
    kept = pl.pallas_call(
        kernel,
        out_shape=[whole] * 3 + [tiles, pltpu.VMEM((16, 128), jnp.int32)],
        in_specs=[hbm] * 6,
        out_specs=[vmem] * 5,
        scratch_shapes=[tiles] * 8
        + [
            pltpu.VMEM((3, 16, COLS), jnp.bfloat16),
            pltpu.VMEM((4, 1, 128), jnp.float32),
            pltpu.VMEM((16, 1, 128), jnp.float32),
            pltpu.VMEM((4, 1, 128), jnp.float32),
            pltpu.VMEM((1, BLOCKS), jnp.int32),
            pltpu.VMEM((1, BLOCKS), jnp.int32),
            pltpu.SMEM((1, BLOCKS), jnp.int32),
            pltpu.SMEM((1, BLOCKS), jnp.int32),
            pltpu.SMEM((16, 128), jnp.int32),
            pltpu.SemaphoreType.DMA((6,)),
            pltpu.SemaphoreType.DMA((2,)),
            pltpu.SemaphoreType.DMA,
            pltpu.SemaphoreType.DMA((3,)),
            pltpu.SemaphoreType.DMA((3,)),
            pltpu.SemaphoreType.DMA((3,)),
            pltpu.SemaphoreType.REGULAR((3,)),
        ],
        compiler_params=pltpu.CompilerParams(
            collective_id=0, has_side_effects=True, vmem_limit_bytes=57 * 2**20
        ),
    )(send_slots, recv_slots, rows_of(moment1_old), rows_of(moment2_old), rows_of(master_old), grad.reshape(3, 16, COLS))
    new = pl.pallas_call(
        finish,
        out_shape=[jax.ShapeDtypeStruct((3, 16, COLS), jnp.float32)] * 3,
        in_specs=[vmem] * 5,
        out_specs=[hbm] * 3,
        scratch_shapes=[whole, pltpu.SMEM((16, 128), jnp.int32), pltpu.SemaphoreType.DMA((6,))],
        compiler_params=pltpu.CompilerParams(vmem_limit_bytes=16 * 2**20),
    )(*kept)
    moment1, moment2, master = [array.reshape(RD, COLS) for array in new]
    return (master, moment1, moment2)


def solution(mesh):
    specs = (P("dp", "tensor"),) * 4 + (P("dp", None),) * 2
    return jax.shard_map(
        per_device, mesh=mesh, in_specs=specs, out_specs=(P("dp", "tensor"),) * 3, check_vma=False
    )
```

time: 137 us -> 130 us (0.949)
  Pallas kernels: 137 us -> 129 us
    pallas_call x1, Pallas kernels: 134 us -> 125 us  [per_device(): pl.pallas_call(kernel, out_shape=[whole] * 3 + [tiles, pltpu.VMEM((16, 12...]
    pallas_call x1, Pallas kernels: 2.41 us -> 4.38 us  [per_device(): pl.pallas_call(finish, out_shape=[jax.ShapeDtypeStruct((3, 16, COLS), jnp...]
where the time goes in v3:
time: 130 us
  Pallas kernels  129 us (99%)
    pallas_call x1, Pallas kernels, per_device(): pl.pallas_call(kernel, out_shape=[whole] * 3 + [tiles, pltpu.VMEM((16, 12...  125 us
    pallas_call x1, Pallas kernels, per_device(): pl.pallas_call(finish, out_shape=[jax.ShapeDtypeStruct((3, 16, COLS), jnp...  4.38 us

profile of v3, /device:TPU:1, one launch (start us, length us, event | category | flops | bytes accessed | tf_op | source)
XLA Modules:
  0.0 130.0 jit_solution(10393265176373537067)
XLA Ops:
  0.6 125.0 %shard_map.85 = (f32[3,16,9216]{2,1,0:T(8,128)S(1)}, f32[3,16,9216]{2,1,0:T(8,128)S(1)}, f32[3,16,9216]{2,1,0:T(8,128)S(1)}, f32[3456,1,128]{2,1,0:T(1,128)S(1)}, s32[16,128]{1,0:T(8,128)S(1)}) custom-call(s32[1,1728]{1,0:T(1,128)} %send_hbm.1, s32[1,1728]{1,0:T(1,128)} %place_hbm.1, f32[3456,1,128]{2,1,0:T(1,128)} %bitcast.19, f32[3456,1,128]{2,1,0:T(1,128)} %bitcast.20, ...), custom_call_target="tpu_custom_call" | custom-call | tf_op jit(solution)/shard_map/pallas_call | solution.py:346
  125.6 4.4 %shard_map.86 = (f32[3,16,9216]{2,1,0:T(8,128)}, f32[3,16,9216]{2,1,0:T(8,128)}, f32[3,16,9216]{2,1,0:T(8,128)}) custom-call(f32[3,16,9216]{2,1,0:T(8,128)S(1)} %get-tuple-element.11.new0, f32[3,16,9216]{2,1,0:T(8,128)S(1)} %get-tuple-element.12.new1, f32[3,16,9216]{2,1,0:T(8,128)S(1)} %get-tuple-element.13.update, ...), custom_call_target="tpu_custom_call" | custom-call | tf_op jit(solution)/shard_map/pallas_call | solution.py:374

commit v4 on v3

--- a/solution.py
+++ b/solution.py
@@ -31,13 +31,15 @@
 
 CHUNK = 512
 EARLY = 3
+FRONT = 21
+BACK = PER_PEER - FRONT
 
 
 def kernel(
     send_hbm, place_hbm, first_hbm, second_hbm, master_hbm, grad_hbm,
-    new0, new1, update, recv2, inverse,
-    old0, old1, old2, send0, send1, send2, recv0, recv1,
-    grad, shard_rows, line_rows, plane_rows, slots, source_rows, send_ref, place_ref, inverse_smem,
+    new0, new1, new2, update, back, back_rows,
+    old0, old1, old2, send0, send1, send2, recv0, recv1, front,
+    grad, shard_rows, line_rows, plane_rows, slots, inverses, send_ref, place_ref, inverse_smem, front_smem,
     load_sems, table_sems, send_sem, recv_sems, small_send, small_recv, entered,
 ):
     me = lax.axis_index("dp")
@@ -45,7 +47,7 @@
     z, x, core = me // 8, (me // 2) % 4, me % 2
     parity = shard % 2
     partner = shard + 1 - 2 * parity
-    olds, sends, recvs = (old0, old1, old2), (send0, send1, send2), (recv0, recv1, recv2)
+    olds, sends = (old0, old1, old2), (send0, send1, send2)
 
     def dp_at(dz, dx, dc):
         return (((z + dz) % 8) * 4 + (x + dx) % 4) * 2 + (core + dc) % 2
@@ -66,25 +68,19 @@
         pltpu.make_async_copy(source, target, load_sems.at[k])
         for k, (source, target) in enumerate(
             [
-                (send_hbm, slots),
+                (send_hbm, send_ref),
                 (first_hbm, old0),
                 (second_hbm, old1),
                 (master_hbm, old2),
                 (grad_hbm, grad),
                 (place_hbm, place_ref),
+                (place_hbm, slots),
             ]
         )
     ]
     for load in loads:
         load.start()
 
-    loads[0].wait()
-    slot = slots[...]
-    row = (slot * 1821) >> 16
-    source_rows[...] = slot * 8 + (row >> 3) * (COLS // 128 * 8) - row * (NSEG * 8) + (row & 7)
-    rows_copy = pltpu.make_async_copy(source_rows, send_ref, table_sems.at[0])
-    rows_copy.start()
-
     def offset_of(n):
         zi = n & 7
         dz = jnp.where((zi & 1) == 0, 4 + (zi >> 1), 3 - (zi >> 1))
@@ -92,16 +88,16 @@
 
     def gather(a, n):
         base = offset_of(n) * PER_PEER
-        rows = [send_ref[0, base + q] for q in range(PER_PEER)]
+        rows = [row_of(send_ref[0, base + q]) for q in range(PER_PEER)]
         for half in range(2):
             tiles = [olds[a][row + half * (NSEG * 8)] for row in rows]
             for q, tile in enumerate(tiles):
                 sends[a][half * BLOCKS + base + q] = tile
 
-    def deliver(a, j, t, half):
+    def deliver(a, j, t, half, target, first=0, count=PER_PEER):
         pltpu.make_async_remote_copy(
-            src_ref=sends[a].at[pl.ds(half * BLOCKS + j * PER_PEER, PER_PEER)],
-            dst_ref=recvs[a].at[pl.ds(parity * BLOCKS + me * PER_PEER, PER_PEER)],
+            src_ref=sends[min(a, 2)].at[pl.ds(half * BLOCKS + j * PER_PEER + first, count)],
+            dst_ref=target.at[pl.ds((parity * N_DP + me) * count, count)],
             send_sem=send_sem,
             recv_sem=recv_sems.at[a],
             device_id=(j, t),
@@ -109,10 +105,10 @@
         ).start()
 
     def deliver_here(a, n):
-        deliver(a, offset_of(n), shard, parity)
+        deliver(a, offset_of(n), shard, parity, recv0)
 
     def deliver_partner(a, n):
-        deliver(a, offset_of(n), partner, 1 - parity)
+        deliver(a, offset_of(n), partner, 1 - parity, recv0)
 
     def gather_and_deliver(first, last):
         @pl.loop(first, last)
@@ -120,7 +116,7 @@
             gather(0, n)
             deliver_here(0, n - 1)
 
-    rows_copy.wait()
+    loads[0].wait()
     loads[1].wait()
 
     @pl.loop(0, EARLY)
@@ -188,10 +184,7 @@
         def _(n):
             gather(a, n)
 
-        own = pl.ds(parity * BLOCKS + me * PER_PEER, PER_PEER)
-        recvs[a][own] = sends[a][own]
-
-    def deliver_all(a):
+    def deliver_all(a, *place):
         def peer(n):
             zi, xi = n & 7, (n >> 3) & 3
             dz = jnp.where((zi & 1) == 0, 4 + (zi >> 1), 3 - (zi >> 1))
@@ -200,19 +193,26 @@
 
         @pl.loop(0, 63)
         def _(n):
-            deliver(a, peer(n), shard, parity)
-            deliver(a, peer(n), partner, 1 - parity)
-
-        deliver(a, me, partner, 1 - parity)
-
-    own = pl.ds(parity * BLOCKS + me * PER_PEER, PER_PEER)
-    recv0[own] = send0[own]
+            deliver(a, peer(n), shard, parity, *place)
+            deliver(a, peer(n), partner, 1 - parity, *place)
+
+        deliver(a, me, partner, 1 - parity, *place)
+
+    def keep(send, target, first=0, count=PER_PEER):
+        target[pl.ds((parity * N_DP + me) * count, count)] = send[
+            pl.ds(parity * BLOCKS + me * PER_PEER + first, count)
+        ]
+
+    keep(send0, recv0)
     loads[2].wait()
     gather_all(1)
+    keep(send1, recv1)
     for k in (1, 2, 3):
         pass_row(0, shard_rows, shard, me, (shard + k) % 4)
     loads[3].wait()
     gather_all(2)
+    keep(send2, front, 0, FRONT)
+    keep(send2, back, FRONT, BACK)
     wait_rows(shard_rows, small_recv.at[0])
     line_rows[z * 2 + core] = sum_of(shard_rows)
 
@@ -223,32 +223,46 @@
     segment = (line - 5 * group) * 8 + (lane >> 4)
     ids = jnp.where((segment < NSEG) & (line < 15), (group * 16 + (lane & 15)) * NSEG + segment, -1)
 
-    def find(n, table):
-        for q in range(16):
-            k = n * 16 + q
-            table = jnp.where(ids == place_ref[0, k], k, table)
-        return table
-
-    inverse[...] = lax.fori_loop(0, BLOCKS // 16, find, jnp.zeros((16, 128), jnp.int32))
-    table_copy = pltpu.make_async_copy(inverse, inverse_smem, table_sems.at[1])
-    table_copy.start()
+    def find(i, tables):
+        whole, part = tables
+        for q in range(PER_PEER):
+            k = i * PER_PEER + q
+            here = ids == place_ref[0, k]
+            whole = jnp.where(here, k, whole)
+            if q < FRONT:
+                part = jnp.where(here, i * FRONT + q, part)
+        return whole, part
+
+    zeros = jnp.zeros((16, 128), jnp.int32)
+    whole, part = lax.fori_loop(0, N_DP, find, (zeros, zeros))
+    inverses[0] = whole
+    inverses[1] = part
+    loads[6].wait()
+    back_rows[...] = row_of(slots[...])
+    table_copies = [
+        pltpu.make_async_copy(inverses.at[0], inverse_smem, table_sems.at[0]),
+        pltpu.make_async_copy(inverses.at[1], front_smem, table_sems.at[1]),
+    ]
+    for copy in table_copies:
+        copy.start()
 
     for k in range(1, 16):
         pass_row(1, line_rows, z * 2 + core, dp_at(k >> 1, 0, k & 1), shard)
-    deliver_all(1)
-    table_copy.wait()
-
-    def arrive(a, new):
-        span = recvs[a].at[pl.ds(0, 127 * PER_PEER)]
+    deliver_all(1, recv1)
+    for copy in table_copies:
+        copy.wait()
+
+    def arrive(a, recv, table, new):
+        span = recv.at[pl.ds(0, recv.shape[0] * 127 // 128)]
         pltpu.make_async_copy(span, span, recv_sems.at[a]).wait()
 
         @pl.loop(0, 12)
         def _(n):
-            place(recvs[a], inverse_smem, new, (n >> 2) * 5 + (n & 3), n >> 2, (n & 3) * 8, 8)
+            place(recv, table, new, (n >> 2) * 5 + (n & 3), n >> 2, (n & 3) * 8, 8)
 
         @pl.loop(0, 3)
         def _(n):
-            place(recvs[a], inverse_smem, new, n * 5 + 4, n, 32, 4)
+            place(recv, table, new, n * 5 + 4, n, 32, 4)
 
     def each_chunk(body):
         @pl.loop(0, 54)
@@ -258,11 +272,12 @@
 
     wait_rows(line_rows, small_recv.at[1])
     plane_rows[x] = sum_of(line_rows)
-    arrive(0, new0)
+    arrive(0, recv0, inverse_smem, new0)
     for k in (1, 2, 3):
         pass_row(2, plane_rows, x, dp_at(0, k, 0), shard)
-    deliver_all(2)
-    arrive(1, new1)
+    deliver_all(2, front, 0, FRONT)
+    deliver_all(3, back, FRONT, BACK)
+    arrive(1, recv1, inverse_smem, new1)
 
     wait_rows(plane_rows, small_recv.at[2])
     total = sum_of(plane_rows)
@@ -283,13 +298,19 @@
 
     each_chunk(first_step)
     each_chunk(second_step)
+    arrive(2, front, front_smem, new2)
     for rows, semaphore in zip((shard_rows, line_rows, plane_rows), range(3), strict=True):
         wait_rows(rows, small_send.at[semaphore])
     for a in range(3):
         span = sends[a].at[pl.ds(0, 127 * PER_PEER)]
         pltpu.make_async_copy(span, span, send_sem).wait()
-    span = recv2.at[pl.ds(0, 127 * PER_PEER)]
-    pltpu.make_async_copy(span, span, recv_sems.at[2]).wait()
+    span = back.at[pl.ds(0, 127 * BACK)]
+    pltpu.make_async_copy(span, span, recv_sems.at[3]).wait()
+
+
+def row_of(slot):
+    row = (slot * 1821) >> 16
+    return slot * 8 + (row >> 3) * (COLS // 128 * 8) - row * (NSEG * 8) + (row & 7)
 
 
 def place(recv, inverse, new, line, group, segment, count):
@@ -297,15 +318,15 @@
         tiles = []
         for r in range(16):
             source = inverse[line, u * 16 + r]
-            tiles.append((recv[source], recv[source + BLOCKS]))
+            tiles.append((recv[source], recv[source + recv.shape[0] // 2]))
         for half in range(2):
             column = pl.ds(pl.multiple_of((half * NSEG + segment + u) * 128, 128), 128)
             for r in range(16):
                 new[group, pl.ds(r, 1), column] = tiles[r][half]
 
 
-def finish(new0, new1, update, recv2, inverse, first_out, second_out, master_out, master, inverse_smem, sems):
-    table = pltpu.make_async_copy(inverse, inverse_smem, sems.at[5])
+def finish(new0, new1, new2, update, back, back_rows, first_out, second_out, master_out, master, rows_smem, sems):
+    table = pltpu.make_async_copy(back_rows, rows_smem, sems.at[5])
     table.start()
     copies = [
         pltpu.make_async_copy(new0, first_out, sems.at[0]),
@@ -313,22 +334,35 @@
     ]
     for copy in copies:
         copy.start()
+
+    @pl.loop(0, TILES // 128)
+    def _(n):
+        rows = pl.ds(pl.multiple_of(n * 128, 128), 128)
+        master[rows, :] = new2[rows, :]
+
     table.wait()
+
+    @pl.loop(0, N_DP // 4)
+    def _(n):
+        for u in range(4):
+            i = n * 4 + u
+            rows = [rows_smem[0, i * PER_PEER + FRONT + q] for q in range(BACK)]
+            for half in range(2):
+                tiles = [back[pl.ds((half * N_DP + i) * BACK + q, 1), :] for q in range(BACK)]
+                for row, tile in zip(rows, tiles, strict=True):
+                    master[pl.ds(row + half * (NSEG * 8), 1), :] = tile
+
+    third = TILES // 3
     for group in range(3):
 
-        @pl.loop(0, 4)
-        def _(n):
-            place(recv2, inverse_smem, master, group * 5 + n, group, n * 8, 8)
-
-        place(recv2, inverse_smem, master, group * 5 + 4, group, 32, 4)
-
-        @pl.loop(0, COLS // CHUNK)
-        def _(n):
-            columns = pl.ds(pl.multiple_of(n * CHUNK, CHUNK), CHUNK)
-            value = master[group, :, columns]
-            master[group, :, columns] = value - learning_rate * (update[group, :, columns] + weight_decay * value)
-
-        copy = pltpu.make_async_copy(master.at[group], master_out.at[group], sems.at[2 + group])
+        @pl.loop(0, third // 128)
+        def _(n):
+            rows = pl.ds(pl.multiple_of(group * third + n * 128, 128), 128)
+            value = master[rows, :]
+            master[rows, :] = value - learning_rate * (update[rows, :] + weight_decay * value)
+
+        span = pl.ds(group * third, third)
+        copy = pltpu.make_async_copy(master.at[span], master_out.at[span], sems.at[2 + group])
         copy.start()
         copies.append(copy)
     for copy in copies:
@@ -343,44 +377,59 @@
     tiles = pltpu.VMEM((TILES, 1, 128), jnp.float32)
     whole = pltpu.VMEM((3, 16, COLS), jnp.float32)
     vmem = pl.BlockSpec(memory_space=pltpu.VMEM)
-    kept = pl.pallas_call(
+    new0, new1, new2, update, back, back_rows = pl.pallas_call(
         kernel,
-        out_shape=[whole] * 3 + [tiles, pltpu.VMEM((16, 128), jnp.int32)],
+        out_shape=[whole] * 4
+        + [pltpu.VMEM((2 * N_DP * BACK, 1, 128), jnp.float32), pltpu.VMEM((1, BLOCKS), jnp.int32)],
         in_specs=[hbm] * 6,
-        out_specs=[vmem] * 5,
+        out_specs=[vmem] * 6,
         scratch_shapes=[tiles] * 8
         + [
+            pltpu.VMEM((2 * N_DP * FRONT, 1, 128), jnp.float32),
             pltpu.VMEM((3, 16, COLS), jnp.bfloat16),
             pltpu.VMEM((4, 1, 128), jnp.float32),
             pltpu.VMEM((16, 1, 128), jnp.float32),
             pltpu.VMEM((4, 1, 128), jnp.float32),
             pltpu.VMEM((1, BLOCKS), jnp.int32),
-            pltpu.VMEM((1, BLOCKS), jnp.int32),
+            pltpu.VMEM((2, 16, 128), jnp.int32),
             pltpu.SMEM((1, BLOCKS), jnp.int32),
             pltpu.SMEM((1, BLOCKS), jnp.int32),
             pltpu.SMEM((16, 128), jnp.int32),
-            pltpu.SemaphoreType.DMA((6,)),
+            pltpu.SMEM((16, 128), jnp.int32),
+            pltpu.SemaphoreType.DMA((7,)),
             pltpu.SemaphoreType.DMA((2,)),
             pltpu.SemaphoreType.DMA,
-            pltpu.SemaphoreType.DMA((3,)),
+            pltpu.SemaphoreType.DMA((4,)),
             pltpu.SemaphoreType.DMA((3,)),
             pltpu.SemaphoreType.DMA((3,)),
             pltpu.SemaphoreType.REGULAR((3,)),
         ],
         compiler_params=pltpu.CompilerParams(
-            collective_id=0, has_side_effects=True, vmem_limit_bytes=57 * 2**20
+            collective_id=0, has_side_effects=True, vmem_limit_bytes=56 * 2**20
         ),
     )(send_slots, recv_slots, rows_of(moment1_old), rows_of(moment2_old), rows_of(master_old), grad.reshape(3, 16, COLS))
     new = pl.pallas_call(
         finish,
-        out_shape=[jax.ShapeDtypeStruct((3, 16, COLS), jnp.float32)] * 3,
-        in_specs=[vmem] * 5,
+        out_shape=[jax.ShapeDtypeStruct((3, 16, COLS), jnp.float32)] * 2
+        + [jax.ShapeDtypeStruct((TILES, 128), jnp.float32)],
+        in_specs=[vmem] * 6,
         out_specs=[hbm] * 3,
-        scratch_shapes=[whole, pltpu.SMEM((16, 128), jnp.int32), pltpu.SemaphoreType.DMA((6,))],
+        scratch_shapes=[
+            pltpu.VMEM((TILES, 128), jnp.float32),
+            pltpu.SMEM((1, BLOCKS), jnp.int32),
+            pltpu.SemaphoreType.DMA((6,)),
+        ],
         compiler_params=pltpu.CompilerParams(vmem_limit_bytes=16 * 2**20),
-    )(*kept)
-    moment1, moment2, master = [array.reshape(RD, COLS) for array in new]
-    return (master, moment1, moment2)
+    )(
+        new0,
+        new1,
+        rows_of(new2).reshape(TILES, 128),
+        rows_of(update).reshape(TILES, 128),
+        back.reshape(2 * N_DP * BACK, 128),
+        back_rows,
+    )
+    master = new[2].reshape(RD // 8, COLS // 128, 8, 128).transpose(0, 2, 1, 3).reshape(RD, COLS)
+    return (master, new[0].reshape(RD, COLS), new[1].reshape(RD, COLS))
 
 
 def solution(mesh):

time: 130 us -> 129 us (level)
  Pallas kernels: 129 us -> 127 us
    pallas_call x1, Pallas kernels: 4.38 us -> 2.58 us  [per_device(): pl.pallas_call(finish, out_shape=[jax.ShapeDtypeStruct((3, 16, COLS), jnp...]
where the time goes in v4:
time: 129 us; the launch traced here: 128 us
  Pallas kernels  127 us (98%)
    pallas_call x1, Pallas kernels, per_device(): pl.pallas_call(kernel, out_shape=[whole] * 4 + [pltpu.VMEM((2 * N_DP * BA...  125 us
    pallas_call x1, Pallas kernels, per_device(): pl.pallas_call(finish, out_shape=[jax.ShapeDtypeStruct((3, 16, COLS), jnp...  2.58 us

profile of v4, /device:TPU:1, one launch (start us, length us, event | category | flops | bytes accessed | tf_op | source)
XLA Modules:
  0.0 128.0 jit_solution(50767844150012594)
XLA Ops:
  0.6 124.8 %shard_map.85 = (f32[3,16,9216]{2,1,0:T(8,128)S(1)}, f32[3,16,9216]{2,1,0:T(8,128)S(1)}, f32[3,16,9216]{2,1,0:T(8,128)S(1)}, f32[3,16,9216]{2,1,0:T(8,128)S(1)},...) custom-call(s32[1,1728]{1,0:T(1,128)} %send_hbm.1, s32[1,1728]{1,0:T(1,128)} %place_hbm.1, f32[3456,1,128]{2,1,0:T(1,128)} %bitcast.37, ...), custom_call_target="tpu_custom_call" | custom-call | tf_op jit(solution)/shard_map/pallas_call | solution.py:380
  125.4 2.6 %shard_map.86 = (f32[3,16,9216]{2,1,0:T(8,128)}, f32[3,16,9216]{2,1,0:T(8,128)}, f32[3456,128]{1,0:T(8,128)}) custom-call(f32[3,16,9216]{2,1,0:T(8,128)S(1)} %get-tuple-element.12.new0, f32[3,16,9216]{2,1,0:T(8,128)S(1)} %get-tuple-element.13.new1, f32[3456,128]{1,0:T(8,128)S(1)} %bitcast.34, f32[3456,128]{1,0:T(8,128)S(1)} %bitcast.35, ...), custom_call_target="tpu_custom_call" | custom-call | tf_op jit(solution)/shard_map/pallas_call | solution.py:411

commit v5 on v4

--- a/solution.py
+++ b/solution.py
@@ -78,7 +78,7 @@
             ]
         )
     ]
-    for load in loads:
+    for load in loads[:2]:
         load.start()
 
     def offset_of(n):
@@ -118,6 +118,8 @@
 
     loads[0].wait()
     loads[1].wait()
+    for load in loads[2:]:
+        load.start()
 
     @pl.loop(0, EARLY)
     def _(n):

time: 129 us -> 129 us (level)
  no operation moved by 1% of the time
where the time goes in v5:
time: 129 us; the launch traced here: 128 us
  Pallas kernels  127 us (98%)
    pallas_call x1, Pallas kernels, per_device(): pl.pallas_call(kernel, out_shape=[whole] * 4 + [pltpu.VMEM((2 * N_DP * BA...  125 us
    pallas_call x1, Pallas kernels, per_device(): pl.pallas_call(finish, out_shape=[jax.ShapeDtypeStruct((3, 16, COLS), jnp...  2.58 us

profile of v5, /device:TPU:1, one launch (start us, length us, event | category | flops | bytes accessed | tf_op | source)
XLA Modules:
  0.0 128.0 jit_solution(2598151501844298574)
XLA Ops:
  0.6 124.8 %shard_map.85 = (f32[3,16,9216]{2,1,0:T(8,128)S(1)}, f32[3,16,9216]{2,1,0:T(8,128)S(1)}, f32[3,16,9216]{2,1,0:T(8,128)S(1)}, f32[3,16,9216]{2,1,0:T(8,128)S(1)},...) custom-call(s32[1,1728]{1,0:T(1,128)} %send_hbm.1, s32[1,1728]{1,0:T(1,128)} %place_hbm.1, f32[3456,1,128]{2,1,0:T(1,128)} %bitcast.37, ...), custom_call_target="tpu_custom_call" | custom-call | tf_op jit(solution)/shard_map/pallas_call | solution.py:382
  125.4 2.6 %shard_map.86 = (f32[3,16,9216]{2,1,0:T(8,128)}, f32[3,16,9216]{2,1,0:T(8,128)}, f32[3456,128]{1,0:T(8,128)}) custom-call(f32[3,16,9216]{2,1,0:T(8,128)S(1)} %get-tuple-element.12.new0, f32[3,16,9216]{2,1,0:T(8,128)S(1)} %get-tuple-element.13.new1, f32[3456,128]{1,0:T(8,128)S(1)} %bitcast.34, f32[3456,128]{1,0:T(8,128)S(1)} %bitcast.35, ...), custom_call_target="tpu_custom_call" | custom-call | tf_op jit(solution)/shard_map/pallas_call | solution.py:413
